TPU v7x, 16 devices: a 4x2x1 block of a 4x4x8 slice. The times are simulated.
16 devices in a mesh: dp: 2 (over y, z), ep: 8 (over x, core).
Axes of the slice: x: 4, y: 2, z: 1, core: 2. Of those that a mesh axis runs over, the one named last changes fastest.
The devices are a block of a 4x4x8 slice.
Arguments:
- tokens: bfloat16 [8192, 2048], P(('dp', 'ep')), parts along dimension 0
- expert_ids: int32 [8192, 6], P(('dp', 'ep')), parts along dimension 0
- gate_vals: float32 [8192, 6], P(('dp', 'ep')), parts along dimension 0
- slots: int32 [8192, 6], P(('dp', 'ep')), parts along dimension 0
- shared_w1: bfloat16 [2048, 2816], replicated
- shared_w3: bfloat16 [2048, 2816], replicated
- shared_w2: bfloat16 [2816, 2048], replicated
- shared_gate: bfloat16 [2048], replicated
- expert_w1: bfloat16 [64, 2048, 1408], P('ep')
- expert_w3: bfloat16 [64, 2048, 1408], P('ep')
- expert_w2: bfloat16 [64, 1408, 2048], P('ep')
Outputs:
- output: bfloat16 [8192, 2048], P(('dp', 'ep')), parts along dimension 0
There are 2 independent parts. A program takes and returns all parts, laid end to end along the dimension named above; an argument that names none is the same for every part.
All inputs are finite; a program needn't handle non-finite values.
Results may differ from a plain program's by a relative error of at most 0.00518217.
Values are sent between devices in bfloat16 or wider.
A program may use at most 768 MiB of HBM per device.

v0:
```python
import functools

import jax
import jax.numpy as jnp
from jax import lax
from jax.experimental import pallas as pl
from jax.experimental.pallas import tpu as pltpu
from jax.sharding import PartitionSpec as P

LANES = 128
STEP = 64
TILE = 128
LOW = 32
PITCH = 24
VMEM_BYTES = 67043328


def chunk_sizes(tok_count):
    quarter = tok_count // 4
    rest = (tok_count - quarter) // 2
    return (quarter, rest, rest)


def router_kernel(sizes, top_k, meta_ref, me_ref, tok_ref, gate_ref, cnt_ref, rank_ref, g_ref):
    num_src = meta_ref.shape[0]
    num_e = rank_ref.shape[0]
    highs = tok_ref.shape[2]
    first = (me_ref[0] * num_e).astype(jnp.float32)
    e_idx = lax.broadcasted_iota(jnp.int32, (num_e, STEP), 0).astype(jnp.float32) + first
    upper = (lax.broadcasted_iota(jnp.int32, (STEP, STEP), 0)
             < lax.broadcasted_iota(jnp.int32, (STEP, STEP), 1)).astype(jnp.float32).astype(jnp.bfloat16)
    start = 0
    for c, size in enumerate(sizes):
        total = num_src * size
        carry = jnp.zeros((num_e, 1), jnp.float32)
        for s in range(num_src):
            for b in range(size // STEP):
                lane0 = start + b * STEP
                mask = jnp.zeros((num_e, STEP), jnp.float32)
                gate = jnp.zeros((num_e, STEP), jnp.float32)
                for k in range(top_k):
                    hit = meta_ref[s, k:k + 1, lane0:lane0 + STEP] == e_idx
                    mask = mask + jnp.where(hit, 1.0, 0.0)
                    gate = gate + jnp.where(hit, meta_ref[s, top_k + k:top_k + k + 1, lane0:lane0 + STEP], 0.0)
                rank = jnp.dot(mask.astype(jnp.bfloat16), upper, preferred_element_type=jnp.float32) + carry
                carry = carry + jnp.sum(mask, axis=1, keepdims=True)
                col = s * size + b * STEP
                rank_ref[:, col:col + STEP] = jnp.where(mask > 0.5, rank, -1.0)
                g_ref[:, col:col + STEP] = gate
        cnt_ref[c] = jnp.broadcast_to(carry, (num_e, LANES)).astype(jnp.int32)
        pos = lax.broadcasted_iota(jnp.int32, (1, total), 1)
        pos_hi = (pos // 64).astype(jnp.float32)
        pos_lo = (pos % 64).astype(jnp.float32)
        hi_iota = lax.broadcasted_iota(jnp.int32, (highs, total), 0).astype(jnp.float32)
        lo_iota = lax.broadcasted_iota(jnp.int32, (LOW, total), 0).astype(jnp.float32)
        slot_iota = (lax.broadcasted_iota(jnp.int32, (highs, LOW), 0) * LOW
                     + lax.broadcasted_iota(jnp.int32, (highs, LOW), 1)).astype(jnp.float32)
        for e in range(num_e):
            rank = rank_ref[e:e + 1, 0:total]
            gate = g_ref[e:e + 1, 0:total]
            hi = jnp.floor(rank * (1.0 / LOW))
            lo = rank - hi * LOW
            in_hi = hi_iota == hi
            in_lo = (lo_iota == lo).astype(jnp.float32).astype(jnp.bfloat16)
            gate_a = gate.astype(jnp.bfloat16).astype(jnp.float32)
            rest = gate - gate_a
            gate_b = rest.astype(jnp.bfloat16).astype(jnp.float32)
            gate_c = rest - gate_b
            left = jnp.concatenate(
                [jnp.where(in_hi, v, 0.0) for v in (pos_hi, pos_lo, gate_a, gate_b, gate_c)], axis=0)
            table = lax.dot_general(left.astype(jnp.bfloat16), in_lo, (((1,), (1,)), ((), ())),
                                    preferred_element_type=jnp.float32)
            tok = table[0:highs] * 64.0 + table[highs:2 * highs]
            live = slot_iota < carry[e:e + 1, 0:1]
            tok_ref[c, e] = jnp.where(live, tok, float(total)).astype(jnp.int32)
            gate_ref[c, e] = table[2 * highs:3 * highs] + (table[3 * highs:4 * highs] + table[4 * highs:5 * highs])
        tok_ref[c, num_e] = jnp.full((highs, LOW), total, jnp.int32)
        gate_ref[c, num_e] = jnp.zeros((highs, LOW), jnp.float32)
        start += size


def route(meta_all, me, sizes, top_k, num_e, rows_max):
    num_src = meta_all.shape[0]
    n_chunks = len(sizes)
    highs = rows_max // LOW
    width = num_src * max(sizes)
    tok, gate, cnt = pl.pallas_call(
        functools.partial(router_kernel, sizes, top_k),
        out_shape=(jax.ShapeDtypeStruct((n_chunks, num_e + 1, highs, LOW), jnp.int32),
                   jax.ShapeDtypeStruct((n_chunks, num_e + 1, highs, LOW), jnp.float32),
                   jax.ShapeDtypeStruct((n_chunks, num_e, LANES), jnp.int32)),
        in_specs=[pl.BlockSpec(memory_space=pltpu.VMEM), pl.BlockSpec(memory_space=pltpu.SMEM)],
        out_specs=(pl.BlockSpec(memory_space=pltpu.VMEM),) * 3,
        scratch_shapes=[pltpu.VMEM((num_e, width), jnp.float32), pltpu.VMEM((num_e, width), jnp.float32)],
        compiler_params=pltpu.CompilerParams(vmem_limit_bytes=32 * 1024 * 1024),
        name="router",
    )(meta_all, me)
    return (tok.reshape(n_chunks, -1), gate.reshape(n_chunks, -1), cnt[:, :, 0])


def ffn_kernel(cnt_ref, tok_ref, gate_ref, x_hbm, w1_hbm, w3_hbm, w2_hbm, out_hbm,
               xv, yf, w1b, w3b, w2b, xg, xb, hb, rg, tile_e, tile_b, in_sem, w_sem, out_sem):
    num_e, hidden, ff = w1_hbm.shape
    rows, subs, _ = x_hbm.shape
    groups = TILE // 8

    def weights(e):
        slot = lax.rem(e, 2)
        return [pltpu.make_async_copy(src.at[e], dst.at[slot], w_sem.at[slot, i])
                for i, (src, dst) in enumerate(((w1_hbm, w1b), (w3_hbm, w3b), (w2_hbm, w2b)))]

    def start_weights(e):
        for copy in weights(e):
            copy.start()

    fetch = pltpu.make_async_copy(x_hbm, xv.at[pl.ds(0, rows)], in_sem)
    fetch.start()
    start_weights(0)
    start_weights(1)

    rows_max = tok_ref.shape[0] // (num_e + 1)
    tile_e[0] = num_e
    tile_b[0] = num_e * rows_max

    def list_expert(e, g):
        def list_tile(i, g):
            tile_e[g] = e
            tile_b[g] = e * rows_max + i * TILE
            return g + 1
        return lax.fori_loop(0, (cnt_ref[e] + TILE - 1) // TILE, list_tile, g)
    end = lax.fori_loop(0, num_e, list_expert, 1)
    tile_e[end] = num_e
    tile_b[end] = num_e * rows_max

    def clear(i, c):
        yf[pl.ds(i * 32, 32)] = jnp.zeros((32, subs, LANES), jnp.float32)
        return c
    lax.fori_loop(0, rows // 32, clear, 0)
    yf[rows] = jnp.zeros((subs, LANES), jnp.float32)
    xv[rows] = jnp.zeros((subs, LANES), jnp.bfloat16)
    fetch.wait()

    def gather(base, i):
        xg[i * PITCH:i * PITCH + subs, :] = xv[tok_ref[base + i]].astype(jnp.float32)

    def pack(j):
        xb[:, j * LANES:(j + 1) * LANES] = xg[pl.ds(j, TILE, stride=PITCH), :].astype(jnp.bfloat16)

    def combine(base, j):
        toks = [tok_ref[base + j * 8 + r] for r in range(8)]
        gates = [gate_ref[base + j * 8 + r] for r in range(8)]
        new = []
        for r in range(8):
            at = (j * 8 + r) * PITCH
            new.append(yf[toks[r]] + gates[r] * rg[at:at + subs, :])
        for r in range(8):
            yf[toks[r]] = new[r]

    for i in range(TILE):
        gather(tile_b[1], i)
    for j in range(subs):
        pack(j)

    def advance(e, c):
        for copy in weights(e):
            copy.wait()

        @pl.when((cnt_ref[e] == 0) & (e + 2 < num_e))
        def _():
            start_weights(e + 2)
        return c

    f_starts = list(range(0, ff, 256))
    d_step = 512
    d_starts = list(range(0, hidden, d_step))

    def one_tile(g, last_e):
        e = tile_e[g]
        lax.fori_loop(last_e + 1, e + 1, advance, 0)
        slot = lax.rem(e, 2)
        prev_b = tile_b[g - 1]
        next_e, next_b = tile_e[g + 1], tile_b[g + 1]
        done = 0
        for i, f in enumerate(f_starts):
            stop = min(f + 256, ff)
            a = jnp.dot(xb[...], w1b[slot, :, f:stop], preferred_element_type=jnp.float32)
            b = jnp.dot(xb[...], w3b[slot, :, f:stop], preferred_element_type=jnp.float32)
            hb[:, f:stop] = (jax.nn.silu(a) * b).astype(jnp.bfloat16)
            goal = groups * (i + 1) // len(f_starts)
            for j in range(done, goal):
                combine(prev_b, j)
            done = goal
        for i in range(TILE):
            gather(next_b, i)
        for d in d_starts:
            r = jnp.dot(hb[...], w2b[slot, :, d:d + d_step], preferred_element_type=jnp.float32)
            r = r.astype(jnp.bfloat16).astype(jnp.float32)
            for j in range(d_step // LANES):
                rg[pl.ds(d // LANES + j, TILE, stride=PITCH), :] = r[:, j * LANES:(j + 1) * LANES]
        for j in range(subs):
            pack(j)

        @pl.when((next_e > e) & (e + 2 < num_e))
        def _():
            start_weights(e + 2)
        return e

    last = lax.fori_loop(1, end, one_tile, -1)
    lax.fori_loop(last + 1, num_e, advance, 0)

    @pl.when(end > 1)
    def _():
        for j in range(groups):
            combine(tile_b[end - 1], j)

    copy = pltpu.make_async_copy(yf.at[pl.ds(0, rows)], out_hbm, out_sem)
    copy.start()
    copy.wait()


def expert_ffn(cnt, tok, gate, x, w1, w3, w2):
    rows, subs, _ = x.shape
    num_e, hidden, ff = w1.shape
    any_spec = pl.BlockSpec(memory_space=pl.ANY)
    smem_spec = pl.BlockSpec(memory_space=pltpu.SMEM)
    max_tiles = tok.shape[0] // TILE + 2
    return pl.pallas_call(
        ffn_kernel,
        out_shape=jax.ShapeDtypeStruct((rows, subs, LANES), jnp.float32),
        in_specs=[smem_spec] * 3 + [any_spec] * 4,
        out_specs=any_spec,
        scratch_shapes=[pltpu.VMEM((rows + 1, subs, LANES), jnp.bfloat16),
                        pltpu.VMEM((rows + 1, subs, LANES), jnp.float32),
                        pltpu.VMEM((2, hidden, ff), jnp.bfloat16),
                        pltpu.VMEM((2, hidden, ff), jnp.bfloat16),
                        pltpu.VMEM((2, ff, hidden), jnp.bfloat16),
                        pltpu.VMEM((TILE * PITCH, LANES), jnp.float32),
                        pltpu.VMEM((TILE, hidden), jnp.bfloat16),
                        pltpu.VMEM((TILE, ff), jnp.bfloat16),
                        pltpu.VMEM((TILE * PITCH, LANES), jnp.float32),
                        pltpu.SMEM((max_tiles,), jnp.int32),
                        pltpu.SMEM((max_tiles,), jnp.int32),
                        pltpu.SemaphoreType.DMA,
                        pltpu.SemaphoreType.DMA((2, 3)),
                        pltpu.SemaphoreType.DMA],
        compiler_params=pltpu.CompilerParams(vmem_limit_bytes=VMEM_BYTES),
        cost_estimate=pl.CostEstimate(flops=6 * rows * hidden * ff, bytes_accessed=6 * num_e * hidden * ff,
                                      transcendentals=0),
        name="expert_ffn",
    )(cnt, tok, gate, x, w1, w3, w2)


def solution(mesh):
    num_ep = mesh.shape['ep']
    row_spec = P(('dp', 'ep'), None)
    replicated = P()
    expert_spec = P('ep', None, None)

    def device_step(tokens, expert_ids, gate_vals, slots, shared_w1, shared_w3, shared_w2, shared_gate, expert_w1, expert_w3, expert_w2):
        tok_count, hidden = tokens.shape
        top_k = expert_ids.shape[1]
        num_e = expert_w1.shape[0]
        num_experts = num_e * num_ep
        capacity = 8 * ((2 * tok_count * top_k + 8 * num_experts - 1) // (8 * num_experts))
        rows_max = num_ep * capacity
        sizes = chunk_sizes(tok_count)
        me = lax.axis_index('ep').astype(jnp.int32).reshape(1)

        kept_ids = jnp.where(slots >= 0, expert_ids, -1).astype(jnp.float32)
        meta = jnp.concatenate([kept_ids, gate_vals], axis=1).T
        meta = jnp.pad(meta, ((0, -meta.shape[0] % 8), (0, 0)))
        meta_all = lax.all_gather(meta, 'ep', axis=0, tiled=False)
        tok, gate, cnt = route(meta_all, me, sizes, top_k, num_e, rows_max)

        start = 0
        subs = hidden // LANES
        tokens3 = tokens.reshape(tok_count, subs, LANES)
        gathered = []
        for size in sizes:
            x = lax.all_gather(tokens3[start:start + size], 'ep', axis=0, tiled=False)
            gathered.append(x.reshape(num_ep * size, subs, LANES))
            start += size

        gate_logit = jnp.dot(tokens, shared_gate, preferred_element_type=jnp.float32)
        shared_a = jnp.dot(tokens, shared_w1, preferred_element_type=jnp.float32)
        shared_b = jnp.dot(tokens, shared_w3, preferred_element_type=jnp.float32)
        shared_h = (jax.nn.silu(shared_a) * shared_b).astype(jnp.bfloat16)
        shared_out = jnp.dot(shared_h, shared_w2, preferred_element_type=jnp.float32)
        base = tokens.astype(jnp.float32) + jax.nn.sigmoid(gate_logit)[:, None] * shared_out

        parts = []
        start = 0
        for c, size in enumerate(sizes):
            partial = expert_ffn(cnt[c], tok[c], gate[c], gathered[c], expert_w1, expert_w3, expert_w2)
            routed = lax.psum_scatter(partial.reshape(num_ep, size, subs, LANES), 'ep', scatter_dimension=0, tiled=False)
            parts.append((base[start:start + size] + routed.reshape(size, hidden)).astype(jnp.bfloat16))
            start += size
        return jnp.concatenate(parts, axis=0)

    return jax.shard_map(device_step, mesh=mesh, in_specs=(row_spec, row_spec, row_spec, row_spec, replicated, replicated, replicated, replicated, expert_spec, expert_spec, expert_spec), out_specs=row_spec, check_vma=False)
```

profile of v0, /device:TPU:112, one launch (start us, length us, event | category | flops | bytes accessed | tf_op | source)
XLA Modules:
  0.0 335.6 jit_solution(4478248681248781986)
XLA Ops:
  6.6 1.1 slice_bitcast_fusion.2
  7.6 0.9 copy.12
  8.6 0.1 all-gather.9.cloned.1.call-start
  8.7 1.5 slice_bitcast_fusion.1
  10.2 1.1 copy.16
  11.4 1.1 copy.14
  12.7 25.4 %all-gather = f32[128,512]{1,0:T(8,128)S(1)} all-gather(f32[16,512]{1,0:T(8,128)S(1)} %pad.4), channel_id=2, replica_groups=mesh['dp'=2,'ep'=8] {'ep'}, dimensions={0}, use_global_device_ids=true | all-gather | bytes 294912 | tf_op jit(solution)/shard_map/all_gather | solution.py:272
  38.1 3.7 %router.1 = (s32[3,9,24,32]{3,2,1,0:T(8,128)S(1)}, f32[3,9,24,32]{3,2,1,0:T(8,128)S(1)}, s32[3,8,128]{2,1,0:T(8,128)S(1)}) custom-call(f32[8,16,512]{2,1,0:T(8,128)S(1)} %bitcast.60, s32[1]{0:T(128)} %bitcast.3.me_ref), custom_call_target="tpu_custom_call" | custom-call | tf_op jit(solution)/shard_map/router/pallas_call | solution.py:87
  41.8 0.7 fusion.4
  42.5 0.7 squeeze.29.tok_ref
  43.2 0.7 fusion.3
  43.9 0.7 squeeze.30.gate_ref
  44.6 0.7 slice_reduce_fusion.2
  45.4 60.4 %expert_ffn.3 = f32[1024,16,128]{2,1,0:T(8,128)} custom-call(s32[8]{0:T(128)} %get-tuple-element.11.cnt_ref, s32[6912]{0:T(1024)} %squeeze.29.tok_ref, f32[6912]{0:T(1024)} %squeeze.30.gate_ref, bf16[1024,16,128]{2,1,0:T(8,128)(2,1)} %bitcast.66, bf16[8,2048,1408]{2,1,0:T(8,128)(2,1)} %w1_hbm.5, bf16[8,2048,1408]{2,1,0:T(8,128)(2,1)} %w3_hbm.5, ...), custom_call_target="tpu_custom_call" | custom-call | flops 17716740096 | bytes 138412032 | tf_op jit(solution)/shard_map/expert_ffn/pallas_call | solution.py:227
  105.9 0.7 copy-done.3
  106.6 0.7 squeeze.35.tok_ref
  107.3 0.7 squeeze.36.gate_ref
  108.0 65.6 %expert_ffn.5 = f32[1536,16,128]{2,1,0:T(8,128)} custom-call(s32[8]{0:T(128)} %get-tuple-element.12.cnt_ref, s32[6912]{0:T(1024)} %squeeze.35.tok_ref, f32[6912]{0:T(1024)} %squeeze.36.gate_ref, bf16[1536,16,128]{2,1,0:T(8,128)(2,1)} %bitcast.65, bf16[8,2048,1408]{2,1,0:T(8,128)(2,1)} %w1_hbm.5, bf16[8,2048,1408]{2,1,0:T(8,128)(2,1)} %w3_hbm.5, ...), custom_call_target="tpu_custom_call" | custom-call | flops 26575110144 | bytes 138412032 | tf_op jit(solution)/shard_map/expert_ffn/pallas_call | solution.py:227
  173.7 0.1 reduce-scatter.6.cloned.1.call-start
  173.7 0.7 copy-done.1
  174.5 0.7 squeeze.32.tok_ref
  175.2 0.7 squeeze.33.gate_ref
  175.9 62.1 %expert_ffn.4 = f32[1536,16,128]{2,1,0:T(8,128)} custom-call(s32[8]{0:T(128)} %get-tuple-element.13.cnt_ref, s32[6912]{0:T(1024)} %squeeze.32.tok_ref, f32[6912]{0:T(1024)} %squeeze.33.gate_ref, bf16[1536,16,128]{2,1,0:T(8,128)(2,1)} %bitcast.64, bf16[8,2048,1408]{2,1,0:T(8,128)(2,1)} %w1_hbm.5, bf16[8,2048,1408]{2,1,0:T(8,128)(2,1)} %w3_hbm.5, ...), custom_call_target="tpu_custom_call" | custom-call | flops 26575110144 | bytes 138412032 | tf_op jit(solution)/shard_map/expert_ffn/pallas_call | solution.py:227
  238.0 0.6 copy-done.8
  238.6 0.9 copy-done
  239.6 0.6 fusion.5
  240.2 11.3 %fusion.6 = f32[512,2816]{1,0:T(8,128)} fusion(bf16[512,2048]{1,0:T(8,128)(2,1)S(1)} %copy-done, bf16[2048,2816]{1,0:T(8,128)(2,1)} %param.15), kind=kOutput, calls=%fused_computation.21 | convolution fusion | flops 5905580032 | bytes 19398656 | tf_op jit(solution)/shard_map/dot_general | solution.py:285
  251.5 23.4 %multiply_add_fusion = f32[512,2048]{1,0:T(8,128)} fusion(bf16[512,2048]{1,0:T(8,128)(2,1)S(1)} %copy-done, bf16[2816,2048]{1,0:T(8,128)(2,1)} %param.17, f32[512]{0:T(512)S(1)} %add_divide_fusion, f32[512,2816]{1,0:T(8,128)} %fusion.6, bf16[2048,2816]{1,0:T(8,128)(2,1)} %param.16), kind=kOutput, calls=%fused_computation.1 | convolution fusion | flops 11822956544 | bytes 35129344 | tf_op jit(solution)/shard_map/dot_general | solution.py:288
  274.9 1.9 fusion.2
  276.9 46.6 %reduce-scatter.6.cloned.1.call-done = f32[1,192,16,128]{3,2,1,0:T(8,128)} async-done(((f32[8,192,16,128]{3,2,1,0:T(8,128)}), f32[1,192,16,128]{3,2,1,0:T(8,128)}) %reduce-scatter.6.cloned.1.call-update) | async-done | bytes 1572880 | tf_op jit(solution)/shard_map/reduce_scatter | solution.py:295
  323.4 3.9 %fusion.1 = (bf16[192,2048]{1,0:T(8,128)(2,1)S(1)}, bf16[192,2048]{1,0:T(8,128)(2,1)S(1)}) fusion(f32[24,8,16,128]{3,2,1,0:T(8,128)} %bitcast.71, f32[512,2048]{1,0:T(8,128)} %multiply_add_fusion, f32[24,8,16,128]{3,2,1,0:T(8,128)} %bitcast.70), kind=kLoop, calls=%fused_computation.6 | loop fusion | flops 1572864 | bytes 7864320 | tf_op jit(solution)/shard_map/convert_element_type | solution.py:296
  327.3 1.5 pad_maximum_fusion
  (34 shorter events, 0.6 us)
Async XLA Ops:
  6.5 38.8 %all-gather.5.cloned.1.call-start = ((), (), s32[]{:S(2)}) async-start(), calls=%async_computation.3 | async-start | bytes 4718592 | tf_op jit(solution)/shard_map/all_gather | solution.py:280
  8.5 4.1 %copy-start.5 = (s32[512,6]{0,1:T(8,128)S(1)}, s32[512,6]{0,1:T(8,128)}, u32[]{:S(2)}) copy-start(s32[512,6]{0,1:T(8,128)} %param.12) | copy-start | bytes 36868
  8.5 4.1 %copy-start.6 = (s32[512,6]{0,1:T(8,128)S(1)}, s32[512,6]{0,1:T(8,128)}, u32[]{:S(2)}) copy-start(s32[512,6]{0,1:T(8,128)} %param.14) | copy-start | bytes 36868
  8.5 4.1 %copy-start.7 = (f32[512,6]{0,1:T(8,128)S(1)}, f32[512,6]{0,1:T(8,128)}, u32[]{:S(2)}) copy-start(f32[512,6]{0,1:T(8,128)} %param.13) | copy-start | bytes 36868
  8.6 99.4 %all-gather.9.cloned.1.call-start = ((), (), s32[]{:S(2)}) async-start(), calls=%async_computation.7 | async-start | bytes 7077888 | tf_op jit(solution)/shard_map/all_gather | solution.py:280
  11.4 164.5 %all-gather.7.cloned.1.call-start = ((), (), s32[]{:S(2)}) async-start(), calls=%async_computation.5 | async-start | bytes 7077888 | tf_op jit(solution)/shard_map/all_gather | solution.py:280
  12.5 262.4 %reduce-scatter.4.cloned.1.call-start = ((), (), s32[]{:S(2)}) async-start(), calls=%async_computation.4 | async-start | bytes 9437184 | tf_op jit(solution)/shard_map/reduce_scatter | solution.py:295
  105.7 0.9 copy-start.3
  105.7 1.6 copy-start.4
  105.8 171.0 %reduce-scatter.8.cloned.1.call-start = ((), (), s32[]{:S(2)}) async-start(), calls=%async_computation.8 | async-start | bytes 14155776 | tf_op jit(solution)/shard_map/reduce_scatter | solution.py:295
  173.6 0.9 copy-start.1
  173.6 1.6 copy-start.2
  173.7 149.8 %reduce-scatter.6.cloned.1.call-start = ((), (), s32[]{:S(2)}) async-start(), calls=%async_computation.6 | async-start | bytes 14155776 | tf_op jit(solution)/shard_map/reduce_scatter | solution.py:295
  237.9 0.7 copy-start.8
  238.0 1.6 copy-start
Sparse Core Ops, SparseCore 0:
  8.9 32.0 all-gather.4
  42.6 36.4 all-gather.8
  80.6 36.6 all-gather.6
  119.4 48.5 reduce-scatter.3
  173.8 74.4 reduce-scatter.7
  250.4 73.0 reduce-scatter.5
where the time goes:
time: 339 us; the launch traced here: 336 us
  Pallas kernels  192 us (57%)
  waiting for transfers between devices  46.9 us (14%)
  matrix products  35.4 us (10%)
  blocking collectives  25.4 us (7%)
  local copies, waits for them, and re-layouts  15 us (4%)
  between operations  13.7 us (4%)
  other arithmetic  7.25 us (2%)
    pallas_call x3, Pallas kernels, expert_ffn(): pl.pallas_call(ffn_kernel, out_shape=jax.ShapeDtypeStruct((rows, subs, LA...  188 us
    reduce_scatter x3, waiting for transfers between devices, device_step(): lax.psum_scatter(partial.reshape(num_ep, size, subs, LANES), 'ep', scatte...  46.6 us
    all_gather x1, blocking collectives, device_step(): meta_all = lax.all_gather(meta, 'ep', axis=0, tiled=False)  25.4 us
    dot_general x1, matrix products, device_step(): jnp.dot(shared_h, shared_w2, preferred_element_type=jnp.float32)  23.4 us
    dot_general x1, matrix products, device_step(): shared_a = jnp.dot(tokens, shared_w1, preferred_element_type=jnp.float32)  11.3 us
    unnamed x24, local copies, waits for them, and re-layouts  8.68 us
  transfers between devices with their start and end apart: 6, of which 1 were waited for; matrix products, arithmetic and copies ran while one was open for 14% of the time, Pallas kernels for 57%

commit v1 on v0

--- a/solution.py
+++ b/solution.py
@@ -18,7 +18,7 @@
 def chunk_sizes(tok_count):
     quarter = tok_count // 4
     rest = (tok_count - quarter) // 2
-    return (quarter, rest, rest)
+    return (rest, rest, quarter)
 
 
 def router_kernel(sizes, top_k, meta_ref, me_ref, tok_ref, gate_ref, cnt_ref, rank_ref, g_ref):

time: 339 us -> 351 us (1.035)
  waiting for transfers between devices: 46.9 us -> 58.5 us
    reduce_scatter x3, waiting for transfers between devices: 46.6 us -> 58.2 us  [device_step(): lax.psum_scatter(partial.reshape(num_ep, size, subs, LANES), 'ep', scatte...]
  transfers between devices with their start and end apart: 6 -> 6, of which waited for: 1 -> 1; matrix products, arithmetic and copies ran while one was open for 14% -> 14% of each run, Pallas kernels for 57% -> 55%
where the time goes in v1:
time: 351 us; the launch traced here: 347 us
  Pallas kernels  192 us (55%)
  waiting for transfers between devices  58.5 us (17%)
  matrix products  35.4 us (10%)
  blocking collectives  25.4 us (7%)
  local copies, waits for them, and re-layouts  15 us (4%)
  between operations  13.7 us (4%)
  other arithmetic  7.25 us (2%)
    pallas_call x3, Pallas kernels, expert_ffn(): pl.pallas_call(ffn_kernel, out_shape=jax.ShapeDtypeStruct((rows, subs, LA...  188 us
    reduce_scatter x3, waiting for transfers between devices, device_step(): lax.psum_scatter(partial.reshape(num_ep, size, subs, LANES), 'ep', scatte...  58.2 us
    all_gather x1, blocking collectives, device_step(): meta_all = lax.all_gather(meta, 'ep', axis=0, tiled=False)  25.4 us
    dot_general x1, matrix products, device_step(): jnp.dot(shared_h, shared_w2, preferred_element_type=jnp.float32)  23.4 us
    dot_general x1, matrix products, device_step(): shared_a = jnp.dot(tokens, shared_w1, preferred_element_type=jnp.float32)  11.3 us
    unnamed x24, local copies, waits for them, and re-layouts  8.7 us
  transfers between devices with their start and end apart: 6, of which 1 were waited for; matrix products, arithmetic and copies ran while one was open for 14% of the time, Pallas kernels for 55%

profile of v1, /device:TPU:112, one launch (start us, length us, event | category | flops | bytes accessed | tf_op | source)
XLA Modules:
  0.0 347.5 jit_solution(2895904807808844261)
XLA Ops:
  6.6 1.1 slice_bitcast_fusion.2
  7.6 0.9 copy.16
  8.6 0.1 all-gather.5.cloned.1.call-start
  8.7 1.5 slice_bitcast_fusion.1
  10.3 1.1 copy.12
  11.4 0.1 all-gather.7.cloned.1.call-start
  11.5 1.0 copy.14
  12.7 25.4 %all-gather = f32[128,512]{1,0:T(8,128)S(1)} all-gather(f32[16,512]{1,0:T(8,128)S(1)} %pad.4), channel_id=2, replica_groups=mesh['dp'=2,'ep'=8] {'ep'}, dimensions={0}, use_global_device_ids=true | all-gather | bytes 294912 | tf_op jit(solution)/shard_map/all_gather | solution.py:272
  38.2 3.7 %router.1 = (s32[3,9,24,32]{3,2,1,0:T(8,128)S(1)}, f32[3,9,24,32]{3,2,1,0:T(8,128)S(1)}, s32[3,8,128]{2,1,0:T(8,128)S(1)}) custom-call(f32[8,16,512]{2,1,0:T(8,128)S(1)} %bitcast.60, s32[1]{0:T(128)} %bitcast.3.me_ref), custom_call_target="tpu_custom_call" | custom-call | tf_op jit(solution)/shard_map/router/pallas_call | solution.py:87
  41.9 0.7 fusion.4
  42.6 0.7 squeeze.35.tok_ref
  43.3 0.7 fusion.3
  44.0 0.7 squeeze.36.gate_ref
  44.7 0.7 slice_reduce_fusion.2
  45.4 57.8 %expert_ffn.5 = f32[1024,16,128]{2,1,0:T(8,128)} custom-call(s32[8]{0:T(128)} %get-tuple-element.12.cnt_ref, s32[6912]{0:T(1024)} %squeeze.35.tok_ref, f32[6912]{0:T(1024)} %squeeze.36.gate_ref, bf16[1024,16,128]{2,1,0:T(8,128)(2,1)} %bitcast.66, bf16[8,2048,1408]{2,1,0:T(8,128)(2,1)} %w1_hbm.5, bf16[8,2048,1408]{2,1,0:T(8,128)(2,1)} %w3_hbm.5, ...), custom_call_target="tpu_custom_call" | custom-call | flops 17716740096 | bytes 138412032 | tf_op jit(solution)/shard_map/expert_ffn/pallas_call | solution.py:227
  103.4 0.7 copy-done.3
  104.1 0.7 squeeze.29.tok_ref
  104.8 0.7 squeeze.30.gate_ref
  105.5 65.4 %expert_ffn.3 = f32[1536,16,128]{2,1,0:T(8,128)} custom-call(s32[8]{0:T(128)} %get-tuple-element.11.cnt_ref, s32[6912]{0:T(1024)} %squeeze.29.tok_ref, f32[6912]{0:T(1024)} %squeeze.30.gate_ref, bf16[1536,16,128]{2,1,0:T(8,128)(2,1)} %bitcast.65, bf16[8,2048,1408]{2,1,0:T(8,128)(2,1)} %w1_hbm.5, bf16[8,2048,1408]{2,1,0:T(8,128)(2,1)} %w3_hbm.5, ...), custom_call_target="tpu_custom_call" | custom-call | flops 26575110144 | bytes 138412032 | tf_op jit(solution)/shard_map/expert_ffn/pallas_call | solution.py:227
  171.0 0.7 copy-done.1
  171.8 0.7 squeeze.32.tok_ref
  172.5 0.7 squeeze.33.gate_ref
  173.2 65.0 %expert_ffn.4 = f32[1536,16,128]{2,1,0:T(8,128)} custom-call(s32[8]{0:T(128)} %get-tuple-element.13.cnt_ref, s32[6912]{0:T(1024)} %squeeze.32.tok_ref, f32[6912]{0:T(1024)} %squeeze.33.gate_ref, bf16[1536,16,128]{2,1,0:T(8,128)(2,1)} %bitcast.64, bf16[8,2048,1408]{2,1,0:T(8,128)(2,1)} %w1_hbm.5, bf16[8,2048,1408]{2,1,0:T(8,128)(2,1)} %w3_hbm.5, ...), custom_call_target="tpu_custom_call" | custom-call | flops 26575110144 | bytes 138412032 | tf_op jit(solution)/shard_map/expert_ffn/pallas_call | solution.py:227
  238.3 0.6 copy-done.8
  238.9 0.9 copy-done
  239.8 0.6 fusion.5
  240.5 11.3 %fusion.6 = f32[512,2816]{1,0:T(8,128)} fusion(bf16[512,2048]{1,0:T(8,128)(2,1)S(1)} %copy-done, bf16[2048,2816]{1,0:T(8,128)(2,1)} %param.15), kind=kOutput, calls=%fused_computation.21 | convolution fusion | flops 5905580032 | bytes 19398656 | tf_op jit(solution)/shard_map/dot_general | solution.py:285
  251.8 23.4 %multiply_add_fusion = f32[512,2048]{1,0:T(8,128)} fusion(bf16[512,2048]{1,0:T(8,128)(2,1)S(1)} %copy-done, bf16[2816,2048]{1,0:T(8,128)(2,1)} %param.17, f32[512]{0:T(512)S(1)} %add_divide_fusion, f32[512,2816]{1,0:T(8,128)} %fusion.6, bf16[2048,2816]{1,0:T(8,128)(2,1)} %param.16), kind=kOutput, calls=%fused_computation.1 | convolution fusion | flops 11822956544 | bytes 35129344 | tf_op jit(solution)/shard_map/dot_general | solution.py:288
  275.2 1.9 fusion.2
  277.1 58.2 %reduce-scatter.6.cloned.1.call-done = f32[1,192,16,128]{3,2,1,0:T(8,128)} async-done(((f32[8,192,16,128]{3,2,1,0:T(8,128)}), f32[1,192,16,128]{3,2,1,0:T(8,128)}) %reduce-scatter.6.cloned.1.call-update) | async-done | bytes 1572880 | tf_op jit(solution)/shard_map/reduce_scatter | solution.py:295
  335.3 3.9 %fusion.1 = (bf16[192,2048]{1,0:T(8,128)(2,1)S(1)}, bf16[192,2048]{1,0:T(8,128)(2,1)S(1)}) fusion(f32[24,8,16,128]{3,2,1,0:T(8,128)} %bitcast.70, f32[512,2048]{1,0:T(8,128)} %multiply_add_fusion, f32[24,8,16,128]{3,2,1,0:T(8,128)} %bitcast.71), kind=kLoop, calls=%fused_computation.6 | loop fusion | flops 1572864 | bytes 7864320 | tf_op jit(solution)/shard_map/convert_element_type | solution.py:296
  339.2 1.5 pad_maximum_fusion
  (34 shorter events, 0.6 us)
Async XLA Ops:
  6.5 38.8 %all-gather.9.cloned.1.call-start = ((), (), s32[]{:S(2)}) async-start(), calls=%async_computation.7 | async-start | bytes 4718592 | tf_op jit(solution)/shard_map/all_gather | solution.py:280
  8.6 4.1 %copy-start.5 = (s32[512,6]{0,1:T(8,128)S(1)}, s32[512,6]{0,1:T(8,128)}, u32[]{:S(2)}) copy-start(s32[512,6]{0,1:T(8,128)} %param.12) | copy-start | bytes 36868
  8.6 4.1 %copy-start.6 = (s32[512,6]{0,1:T(8,128)S(1)}, s32[512,6]{0,1:T(8,128)}, u32[]{:S(2)}) copy-start(s32[512,6]{0,1:T(8,128)} %param.14) | copy-start | bytes 36868
  8.6 4.1 %copy-start.7 = (f32[512,6]{0,1:T(8,128)S(1)}, f32[512,6]{0,1:T(8,128)}, u32[]{:S(2)}) copy-start(f32[512,6]{0,1:T(8,128)} %param.13) | copy-start | bytes 36868
  8.6 96.9 %all-gather.5.cloned.1.call-start = ((), (), s32[]{:S(2)}) async-start(), calls=%async_computation.3 | async-start | bytes 7077888 | tf_op jit(solution)/shard_map/all_gather | solution.py:280
  11.4 161.8 %all-gather.7.cloned.1.call-start = ((), (), s32[]{:S(2)}) async-start(), calls=%async_computation.5 | async-start | bytes 7077888 | tf_op jit(solution)/shard_map/all_gather | solution.py:280
  12.6 262.6 %reduce-scatter.8.cloned.1.call-start = ((), (), s32[]{:S(2)}) async-start(), calls=%async_computation.8 | async-start | bytes 9437184 | tf_op jit(solution)/shard_map/reduce_scatter | solution.py:295
  103.2 0.9 copy-start.3
  103.2 1.6 copy-start.4
  103.3 173.8 %reduce-scatter.4.cloned.1.call-start = ((), (), s32[]{:S(2)}) async-start(), calls=%async_computation.4 | async-start | bytes 14155776 | tf_op jit(solution)/shard_map/reduce_scatter | solution.py:295
  170.9 0.9 copy-start.1
  170.9 1.6 copy-start.2
  171.0 164.3 %reduce-scatter.6.cloned.1.call-start = ((), (), s32[]{:S(2)}) async-start(), calls=%async_computation.6 | async-start | bytes 14155776 | tf_op jit(solution)/shard_map/reduce_scatter | solution.py:295
  238.2 0.7 copy-start.8
  238.2 1.6 copy-start
Sparse Core Ops, SparseCore 0:
  8.9 32.0 all-gather.8
  42.6 36.3 all-gather.4
  80.6 36.6 all-gather.6
  119.4 48.5 reduce-scatter.7
  171.1 87.1 reduce-scatter.3
  260.4 74.8 reduce-scatter.5
